TPU v7x, 32 devices: a whole 2x2x4 slice. The times are simulated.
32 devices in a mesh: subj: 8 (over y, x, core), feat: 4 (over z).
Axes of the slice: x: 2, y: 2, z: 4, core: 2. Of those that a mesh axis runs over, the one named last changes fastest.
Arguments:
- records: float32 [8192, 16384], P('subj', 'feat'), may hold values from -6 to 6
- feature_factor: float32 [16384, 64], P('feat'), may hold values from -0.046875 to 0.046875
- mixing: float32 [64, 64], replicated, may hold values from -0.75 to 0.75
- weights: float32 [32, 64], P('subj'), may hold values from 0.3 to 3
- visits: int32 [32], P('subj'), may hold values from 128 to 640, as said below
Outputs:
- new_factor: float32 [16384, 64], P('feat')
- new_mixing: float32 [64, 64], replicated
- new_weights: float32 [32, 64], P('subj')
Inputs may be any that keep to these rules, and one draw needn't show every extreme that they name: The visits of subjects b * 4 to b * 4 + 3 sum to 1024 for every b.
All inputs are finite; a program needn't handle non-finite values.
Results may differ from a plain program's by a relative error of at most 0.0005.
Values sent between devices are 32-bit elements; how exact they have to be, the bound alone decides.
A program may use at most 64 MiB of HBM per device.

v0:
```python
import jax
import jax.numpy as jnp
from jax import lax
from jax.sharding import PartitionSpec as P

ITERS = 3
NS_ITERS = 8


HIGH = lax.Precision.HIGHEST


def slot_table(counts, rows):
    ends = jnp.cumsum(counts)
    starts = ends - counts
    position = lax.broadcasted_iota(jnp.int32, (rows, counts.shape[0]), 0)
    return ((position >= starts[None, :]) & (position < ends[None, :])).astype(jnp.float32)


def inverse_root(gram):
    size = gram.shape[-1]
    scale = jnp.trace(gram, axis1=1, axis2=2) + 1e-06
    ident = jnp.broadcast_to(jnp.eye(size, dtype=jnp.float32), gram.shape)
    upper = gram / scale[:, None, None]
    lower = ident
    for step in range(NS_ITERS):
        middle = 1.5 * ident - 0.5 * jnp.einsum("kab,kbc->kac", lower, upper, precision=HIGH)
        upper, lower = (
            jnp.einsum("kab,kbc->kac", upper, middle, precision=HIGH),
            jnp.einsum("kab,kbc->kac", middle, lower, precision=HIGH),
        )
    return lower / jnp.sqrt(scale)[:, None, None]


def solve_gram(gram, rhs):
    factor = jnp.linalg.cholesky(gram)
    return jax.scipy.linalg.cho_solve((factor, True), rhs.T).T


def per_device(records, feature_factor, mixing, weights, visits):
    row_count = records.shape[0]
    slots = slot_table(visits, row_count)
    factor, mix, wts = (feature_factor, mixing, weights)
    for outer in range(ITERS):
        local_proj = jnp.dot(records, factor, precision=HIGH, preferred_element_type=jnp.float32)
        local_vgram = jnp.dot(factor.T, factor, precision=HIGH, preferred_element_type=jnp.float32)
        proj, vgram = lax.psum((local_proj, local_vgram), "feat")
        wrow = jnp.dot(slots, wts, precision=HIGH, preferred_element_type=jnp.float32)
        mixed = jnp.einsum("nr,qr->nq", proj * wrow, mix, precision=HIGH)
        spread = slots[:, :, None] * mixed[:, None, :]
        gram = jnp.einsum("nsr,nq->srq", spread, mixed, precision=HIGH)
        cross = jnp.einsum("nsr,nq->srq", spread, proj, precision=HIGH)
        root = inverse_root(gram)
        core = jnp.einsum("krq,kqp->krp", root, cross, precision=HIGH)
        local_msum = jnp.einsum("krq,kq->rq", core, wts, precision=HIGH)
        local_wgram = jnp.dot(wts.T, wts, precision=HIGH, preferred_element_type=jnp.float32)
        msum, wgram = lax.psum((local_msum, local_wgram), "subj")
        mix_new = solve_gram(vgram * wgram, msum)
        hgram = jnp.dot(mix_new.T, mix_new, precision=HIGH, preferred_element_type=jnp.float32)
        wtarget = jnp.einsum("rq,krq->kq", mix_new, core, precision=HIGH)
        wts_new = solve_gram(hgram * vgram, wtarget)
        rotated = jnp.einsum("nr,srq->nsq", mixed, root, precision=HIGH)
        ortho = jnp.sum(rotated * slots[:, :, None], axis=1)
        wrow_new = jnp.dot(slots, wts_new, precision=HIGH, preferred_element_type=jnp.float32)
        basis = (
            jnp.dot(ortho, mix_new, precision=HIGH, preferred_element_type=jnp.float32) * wrow_new
        )
        local_wgram_new = jnp.dot(
            wts_new.T, wts_new, precision=HIGH, preferred_element_type=jnp.float32
        )
        local_total = jnp.einsum("nj,nr->jr", records, basis, precision=HIGH)
        total, wgram_new = lax.psum((local_total, local_wgram_new), "subj")
        factor = solve_gram(hgram * wgram_new, total)
        mix, wts = (mix_new, wts_new)
    return (factor, mix, wts)


def solution(mesh):
    placed = (P("subj", "feat"), P("feat", None), P(), P("subj", None), P("subj"))
    return jax.shard_map(
        per_device,
        mesh=mesh,
        in_specs=placed,
        out_specs=(P("feat", None), P(), P("subj", None)),
        check_vma=False,
    )
```

profile of v0, /device:TPU:0, one launch (start us, length us, event | category | flops | bytes accessed | tf_op | source)
XLA Modules:
  0.0 574.2 jit_solution(13154702220031810701)
XLA Ops:
  7.3 1.1 copy-done
  8.4 20.4 %fusion.163 = f32[1024,64]{0,1:T(8,128)} fusion(f32[1024,4096]{1,0:T(8,128)} %param.12, f32[4096,64]{0,1:T(8,128)S(1)} %copy-done), kind=kOutput, calls=%fused_computation.241 | convolution fusion | flops 3221225472 | bytes 18087936 | tf_op jit(solution)/shard_map/dot_general | solution.py:45
  28.9 1.0 fusion.161
  30.2 21.5 %psum.118 = f32[64,64]{0,1:T(8,128)S(1)} all-reduce(f32[64,64]{0,1:T(8,128)S(1)} %fusion.161), channel_id=1, replica_groups=mesh['subj'=8,'feat'=4] {'feat'}, use_global_device_ids=true, to_apply=%region_0.0 | all-reduce | flops 4096 | bytes 32768 | tf_op jit(solution)/shard_map/psum | solution.py:47
  51.9 15.7 %all-reduce.8.cloned.1.call-done = f32[1024,64]{0,1:T(8,128)} async-done(((f32[1024,64]{0,1:T(8,128)}), f32[1024,64]{0,1:T(8,128)}) %all-reduce.8.cloned.1.call-update) | async-done | bytes 262160 | tf_op jit(solution)/shard_map/psum | solution.py:47
  67.6 1.3 convolution_multiply_fusion.6
  69.3 1.1 select_reduce_fusion.2
  76.6 1.0 fusion.12
  77.6 1.9 fusion.8
  80.0 23.2 %all-reduce = (f32[64,64]{1,0:T(8,128)S(1)}, f32[64,64]{0,1:T(8,128)S(1)}) all-reduce(f32[64,64]{1,0:T(8,128)S(1)} %copy.62, f32[64,64]{0,1:T(8,128)S(1)} %fusion.162), channel_id=1, replica_groups=mesh['subj'=8,'feat'=4] {'subj'}, use_global_device_ids=true, to_apply=%region_7.9 | all-reduce | flops 8192 | bytes 65536 | tf_op jit(solution)/shard_map/psum | solution.py:57
  103.3 5.8 %cholesky.149 = f32[64,64]{1,0:T(8,128)S(1)} custom-call(f32[64,64]{1,0:T(8,128)S(1)} %fusion.125), custom_call_target="Cholesky" | custom-call | tf_op jit(solution)/shard_map/jit(cholesky)/cholesky | solution.py:36
  110.5 4.9 custom-call.23
  116.1 5.8 %cholesky.160 = f32[64,64]{1,0:T(8,128)S(1)} custom-call(f32[64,64]{1,0:T(8,128)S(1)} %fusion.120), custom_call_target="Cholesky" | custom-call | tf_op jit(solution)/shard_map/jit(cholesky)/cholesky | solution.py:36
  123.3 4.9 custom-call.24
  130.2 14.7 %fusion.179 = f32[64,4096]{1,0:T(8,128)} fusion(f32[1024,64]{0,1:T(8,128)S(1)} %convolution_multiply_fusion.5, f32[1024,4096]{1,0:T(8,128)} %param.12), kind=kOutput, calls=%fused_computation.257 | convolution fusion | flops 3221225472 | bytes 18087936 | tf_op jit(solution)/shard_map/nj,nr->jr/dot_general | solution.py:71
  145.0 22.7 %psum.122 = f32[64,64]{0,1:T(8,128)S(1)} all-reduce(f32[64,64]{0,1:T(8,128)S(1)} %fusion.178), channel_id=1, replica_groups=mesh['subj'=8,'feat'=4] {'subj'}, use_global_device_ids=true, to_apply=%region_8.12 | all-reduce | flops 4096 | bytes 32768 | tf_op jit(solution)/shard_map/psum | solution.py:72
  167.7 5.9 %cholesky.171 = f32[64,64]{1,0:T(8,128)S(1)} custom-call(f32[64,64]{1,0:T(8,128)S(1)} %fusion.115), custom_call_target="Cholesky" | custom-call | tf_op jit(solution)/shard_map/jit(cholesky)/cholesky | solution.py:36
  174.9 4.9 custom-call.25
  179.8 21.4 %all-reduce.10.cloned.1.call-done = f32[64,4096]{1,0:T(8,128)} async-done(((f32[64,4096]{1,0:T(8,128)}), f32[64,4096]{1,0:T(8,128)}) %all-reduce.10.cloned.1.call-update) | async-done | bytes 1048592 | tf_op jit(solution)/shard_map/psum | solution.py:72
  201.2 2.2 fusion.113
  203.5 1.0 fusion.111
  204.5 20.2 %convolution_bitcast_fusion.2 = f32[1024,64]{0,1:T(8,128)} fusion(f32[64,4096]{1,0:T(8,128)S(1)} %fusion.111, f32[1024,4096]{1,0:T(8,128)} %param.12), kind=kOutput, calls=%fused_computation.24 | convolution fusion | flops 3221225472 | bytes 18087936 | tf_op jit(solution)/shard_map/dot_general | solution.py:45
  224.7 1.0 fusion.180
  225.7 19.3 %psum.124 = f32[64,64]{0,1:T(8,128)S(1)} all-reduce(f32[64,64]{0,1:T(8,128)S(1)} %fusion.180), channel_id=1, replica_groups=mesh['subj'=8,'feat'=4] {'feat'}, use_global_device_ids=true, to_apply=%region_11.16 | all-reduce | flops 4096 | bytes 32768 | tf_op jit(solution)/shard_map/psum | solution.py:47
  245.1 5.8 %cholesky.182 = f32[64,64]{1,0:T(8,128)S(1)} custom-call(f32[64,64]{1,0:T(8,128)S(1)} %fusion.110), custom_call_target="Cholesky" | custom-call | tf_op jit(solution)/shard_map/jit(cholesky)/cholesky | solution.py:36
  252.3 4.9 custom-call.26
  257.2 3.8 all-reduce.12.cloned.1.call-done
  261.1 1.4 fusion.62
  262.4 1.1 select_reduce_fusion.1
  269.7 1.0 fusion.13
  270.8 1.9 fusion.4
  273.0 23.2 %psum.126 = f32[64,64]{1,0:T(8,128)S(1)} all-reduce(f32[64,64]{1,0:T(8,128)S(1)} %copy.75), channel_id=1, replica_groups=mesh['subj'=8,'feat'=4] {'subj'}, use_global_device_ids=true, to_apply=%region_14.19 | all-reduce | flops 4096 | bytes 32768 | tf_op jit(solution)/shard_map/psum | solution.py:57
  297.0 5.8 %cholesky.193 = f32[64,64]{1,0:T(8,128)S(1)} custom-call(f32[64,64]{1,0:T(8,128)S(1)} %fusion.105), custom_call_target="Cholesky" | custom-call | tf_op jit(solution)/shard_map/jit(cholesky)/cholesky | solution.py:36
  304.2 4.9 custom-call.27
  311.1 14.7 %fusion.195 = f32[64,4096]{1,0:T(8,128)} fusion(f32[1024,64]{0,1:T(8,128)S(1)} %convolution_multiply_fusion.4, f32[1024,4096]{1,0:T(8,128)} %param.12), kind=kOutput, calls=%fused_computation.273 | convolution fusion | flops 3221225472 | bytes 18087936 | tf_op jit(solution)/shard_map/nj,nr->jr/dot_general | solution.py:71
  325.9 22.7 %psum.127 = f32[64,64]{0,1:T(8,128)S(1)} all-reduce(f32[64,64]{0,1:T(8,128)S(1)} %fusion.194), channel_id=1, replica_groups=mesh['subj'=8,'feat'=4] {'subj'}, use_global_device_ids=true, to_apply=%region_15.20 | all-reduce | flops 4096 | bytes 32768 | tf_op jit(solution)/shard_map/psum | solution.py:72
  348.7 5.8 %cholesky.204 = f32[64,64]{1,0:T(8,128)S(1)} custom-call(f32[64,64]{1,0:T(8,128)S(1)} %fusion.100), custom_call_target="Cholesky" | custom-call | tf_op jit(solution)/shard_map/jit(cholesky)/cholesky | solution.py:36
  355.9 4.9 custom-call.28
  360.8 20.6 %all-reduce.14.cloned.1.call-done = f32[64,4096]{1,0:T(8,128)} async-done(((f32[64,4096]{1,0:T(8,128)}), f32[64,4096]{1,0:T(8,128)}) %all-reduce.14.cloned.1.call-update) | async-done | bytes 1048592 | tf_op jit(solution)/shard_map/psum | solution.py:72
  381.4 2.2 fusion.98
  383.6 1.0 fusion.96
  384.7 20.2 %convolution_bitcast_fusion.1 = f32[1024,64]{0,1:T(8,128)} fusion(f32[64,4096]{1,0:T(8,128)S(1)} %fusion.96, f32[1024,4096]{1,0:T(8,128)} %param.12), kind=kOutput, calls=%fused_computation.23 | convolution fusion | flops 3221225472 | bytes 18087936 | tf_op jit(solution)/shard_map/dot_general | solution.py:45
  404.8 1.0 fusion.196
  405.9 19.3 %psum.129 = f32[64,64]{0,1:T(8,128)S(1)} all-reduce(f32[64,64]{0,1:T(8,128)S(1)} %fusion.196), channel_id=1, replica_groups=mesh['subj'=8,'feat'=4] {'feat'}, use_global_device_ids=true, to_apply=%region_18.23 | all-reduce | flops 4096 | bytes 32768 | tf_op jit(solution)/shard_map/psum | solution.py:47
  425.3 5.8 %cholesky.215 = f32[64,64]{1,0:T(8,128)S(1)} custom-call(f32[64,64]{1,0:T(8,128)S(1)} %fusion.95), custom_call_target="Cholesky" | custom-call | tf_op jit(solution)/shard_map/jit(cholesky)/cholesky | solution.py:36
  432.5 4.9 custom-call.29
  437.4 3.7 all-reduce.16.cloned.1.call-done
  441.0 1.4 fusion.60
  442.4 1.1 select_reduce_fusion
  449.7 1.0 fusion.14
  450.7 1.9 fusion
  453.0 22.6 %psum.131 = f32[64,64]{1,0:T(8,128)S(1)} all-reduce(f32[64,64]{1,0:T(8,128)S(1)} %copy.88), channel_id=1, replica_groups=mesh['subj'=8,'feat'=4] {'subj'}, use_global_device_ids=true, to_apply=%region_21.26 | all-reduce | flops 4096 | bytes 32768 | tf_op jit(solution)/shard_map/psum | solution.py:57
  476.2 1.0 fusion.211
  477.4 5.8 %cholesky.226 = f32[64,64]{1,0:T(8,128)S(1)} custom-call(f32[64,64]{1,0:T(8,128)S(1)} %fusion.90), custom_call_target="Cholesky" | custom-call | tf_op jit(solution)/shard_map/jit(cholesky)/cholesky | solution.py:36
  484.6 4.9 custom-call.30
  490.8 0.7 convolution_multiply_fusion.3
  491.5 14.7 %fusion.212 = f32[64,4096]{1,0:T(8,128)} fusion(f32[1024,64]{1,0:T(8,128)S(1)} %convolution_multiply_fusion.3, f32[1024,4096]{1,0:T(8,128)} %param.12), kind=kOutput, calls=%fused_computation.290 | convolution fusion | flops 3221225472 | bytes 18087936 | tf_op jit(solution)/shard_map/nj,nr->jr/dot_general | solution.py:71
  506.2 22.8 %psum.132 = f32[64,64]{0,1:T(8,128)S(1)} all-reduce(f32[64,64]{0,1:T(8,128)S(1)} %fusion.210), channel_id=1, replica_groups=mesh['subj'=8,'feat'=4] {'subj'}, use_global_device_ids=true, to_apply=%region_22.27 | all-reduce | flops 4096 | bytes 32768 | tf_op jit(solution)/shard_map/psum | solution.py:72
  529.1 5.9 %cholesky.237 = f32[64,64]{1,0:T(8,128)S(1)} custom-call(f32[64,64]{1,0:T(8,128)S(1)} %fusion.85), custom_call_target="Cholesky" | custom-call | tf_op jit(solution)/shard_map/jit(cholesky)/cholesky | solution.py:36
  536.3 4.9 custom-call.31
  541.2 0.7 copy.53
  541.9 20.7 %all-reduce.18.cloned.1.call-done = f32[64,4096]{1,0:T(8,128)} async-done(((f32[64,4096]{1,0:T(8,128)}), f32[64,4096]{1,0:T(8,128)}) %all-reduce.18.cloned.1.call-update) | async-done | bytes 1048592 | tf_op jit(solution)/shard_map/psum | solution.py:72
  562.6 2.2 fusion.83
  564.9 2.0 convolution_bitcast_fusion
  (186 shorter events, 40.4 us)
Async XLA Ops:
  7.2 1.2 copy-start
  7.2 22.7 %copy-start.4 = (s32[4]{0:T(128)S(1)}, s32[4]{0:T(128)}, u32[]{:S(2)}) copy-start(s32[4]{0:T(128)} %param.16) | copy-start | bytes 52
  7.2 44.5 %copy-start.2 = (f32[4,64]{1,0:T(4,128)S(1)}, f32[4,64]{1,0:T(4,128)}, u32[]{:S(2)}) copy-start(f32[4,64]{1,0:T(4,128)} %param.15) | copy-start | bytes 3076
  7.2 61.7 %copy-start.1 = (f32[64,64]{1,0:T(8,128)S(1)}, f32[64,64]{1,0:T(8,128)}, u32[]{:S(2)}) copy-start(f32[64,64]{1,0:T(8,128)} %param.14) | copy-start | bytes 49156
  7.2 60.4 %all-reduce.8.cloned.1.call-start = ((), (), s32[]{:S(2)}) async-start(), calls=%async_computation | async-start | bytes 524288 | tf_op jit(solution)/shard_map/psum | solution.py:47
  28.9 172.4 %all-reduce.10.cloned.1.call-start = ((), (), s32[]{:S(2)}) async-start(), calls=%async_computation.1 | async-start | bytes 2097152 | tf_op jit(solution)/shard_map/psum | solution.py:72
  144.9 116.2 %all-reduce.12.cloned.1.call-start = ((), (), s32[]{:S(2)}) async-start(), calls=%async_computation.2 | async-start | bytes 524288 | tf_op jit(solution)/shard_map/psum | solution.py:47
  225.7 155.7 %all-reduce.14.cloned.1.call-start = ((), (), s32[]{:S(2)}) async-start(), calls=%async_computation.3 | async-start | bytes 2097152 | tf_op jit(solution)/shard_map/psum | solution.py:72
  325.8 115.2 %all-reduce.16.cloned.1.call-start = ((), (), s32[]{:S(2)}) async-start(), calls=%async_computation.4 | async-start | bytes 524288 | tf_op jit(solution)/shard_map/psum | solution.py:47
  405.8 156.8 %all-reduce.18.cloned.1.call-start = ((), (), s32[]{:S(2)}) async-start(), calls=%async_computation.5 | async-start | bytes 2097152 | tf_op jit(solution)/shard_map/psum | solution.py:72
  490.5 76.3 %copy-start.3 = (f32[64,4]{0,1:T(4,128)}, f32[64,4]{0,1:T(4,128)S(1)}, u32[]{:S(2)}) copy-start(f32[64,4]{0,1:T(4,128)S(1)} %fusion.86) | copy-start | bytes 3076
Sparse Core Ops, SparseCore 0:
  29.0 38.5 all-reduce.7
  145.0 56.1 all-reduce.9
  225.8 35.2 all-reduce.11
  325.9 55.4 all-reduce.13
  405.9 35.0 all-reduce.15
  506.3 56.2 all-reduce.17
where the time goes:
time: 580 us; the launch traced here: 574 us
  blocking collectives  197 us (34%)
  matrix products  163 us (28%)
  other arithmetic  109 us (19%)
  waiting for transfers between devices  86 us (15%)
  between operations  15.9 us (3%)
    psum x3, blocking collectives, per_device(): msum, wgram = lax.psum((local_msum, local_wgram), 'subj')  69 us
    psum x3, blocking collectives, per_device(): total, wgram_new = lax.psum((local_total, local_wgram_new), 'subj')  68.2 us
    psum x3, waiting for transfers between devices, per_device(): total, wgram_new = lax.psum((local_total, local_wgram_new), 'subj')  62.7 us
    dot_general x3, matrix products, per_device(): jnp.dot(records, factor, precision=HIGH, preferred_element_type=jnp.float32)  60.7 us
    psum x3, blocking collectives, per_device(): proj, vgram = lax.psum((local_proj, local_vgram), 'feat')  60.1 us
    another operation x28, other arithmetic, solve_gram(): factor = jnp.linalg.cholesky(gram)  58.7 us
    another operation x18, other arithmetic, solve_gram(): return jax.scipy.linalg.cho_solve((factor, True), rhs.T).T  49.9 us
    dot_general x3, matrix products, per_device(): local_total = jnp.einsum('nj,nr->jr', records, basis, precision=HIGH)  44 us
  transfers between devices with their start and end apart: 6, of which 6 were waited for; matrix products, arithmetic and copies ran while one was open for 11% of the time, Pallas kernels for 0%

commit v1 on v0

v1 whole, which is shorter than its diff:
```python
import functools

import jax
import jax.numpy as jnp
from jax import lax
from jax.experimental import pallas as pl
from jax.experimental.pallas import tpu as pltpu
from jax.sharding import PartitionSpec as P

ITERS = 3
NS_ITERS = 8
SUBLANES = 8
HIGH = lax.Precision.HIGHEST
BIG = lax.Precision.HIGH
MESH = pl.DeviceIdType.MESH
F32 = jnp.float32


def slot_rows(counts, rows, padded):
    ends = jnp.cumsum(counts)
    starts = ends - counts
    position = lax.broadcasted_iota(jnp.int32, (counts.shape[0], rows), 1)
    mask = ((position >= starts[:, None]) & (position < ends[:, None])).astype(F32)
    return jnp.pad(mask, ((0, padded - counts.shape[0]), (0, 0)))


def dot(a, b, dims=((1,), (0,))):
    return lax.dot_general(a, b, (dims, ((), ())), precision=HIGH, preferred_element_type=F32)


TN = ((0,), (0,))
NT = ((1,), (1,))


def spd_inverse(a):
    size = a.shape[0]
    row_id = lax.broadcasted_iota(jnp.int32, a.shape, 0)
    col_id = lax.broadcasted_iota(jnp.int32, a.shape, 1)
    for k in range(size):
        col = a[:, k : k + 1]
        scale = 1.0 / a[k : k + 1, k : k + 1]
        a = jnp.where(col_id == k, (row_id == k).astype(F32), a)
        row = a[k : k + 1, :] * scale
        a = jnp.where(row_id == k, row, a - col * row)
    return a


def peer_of(axis, n, k):
    return lax.rem(lax.axis_index(axis) + k, n)


def greet(groups):
    barrier = pltpu.get_barrier_semaphore()
    count = 0
    for axis, n in groups:
        for k in range(1, n):
            pl.semaphore_signal(barrier, inc=1, device_id={axis: peer_of(axis, n, k)}, device_id_type=MESH)
            count += 1
    if count:
        pl.semaphore_wait(barrier, count)


def send_all(src_of, dst_of, sems, axis, n):
    copies = []
    for k in range(1, n):
        peer = peer_of(axis, n, k)
        copy = pltpu.make_async_remote_copy(
            src_ref=src_of(peer),
            dst_ref=dst_of(k),
            send_sem=sems.at[0, k - 1],
            recv_sem=sems.at[1, k - 1],
            device_id={axis: peer},
            device_id_type=MESH,
        )
        copy.start()
        copies.append(copy)
    return copies


def wait_recv(copies):
    for copy in copies:
        copy.wait_recv()


def wait_send(copies):
    for copy in copies:
        copy.wait_send()


def chunk(index, size):
    return pl.ds(pl.multiple_of(index * size, SUBLANES), size)


def scatter_start(x_ref, part, sems, axis, n):
    size = x_ref.shape[0] // n
    return send_all(lambda peer: x_ref.at[chunk(peer, size)], lambda k: part.at[k - 1], sems, axis, n)


def scatter_finish(x_ref, copies, part, mine, full, sems, axis, n):
    size = x_ref.shape[0] // n
    me = lax.axis_index(axis)
    wait_recv(copies)
    acc = x_ref[chunk(me, size), :]
    for k in range(1, n):
        acc = acc + part[k - 1]
    mine[...] = acc
    gather = send_all(lambda peer: mine, lambda k: full.at[chunk(me, size)], sems, axis, n)
    full[chunk(me, size), :] = acc
    wait_recv(gather)
    wait_send(copies)
    wait_send(gather)


def exchange_start(src, slots, sems, axis, n):
    return send_all(lambda peer: src, lambda k: slots.at[lax.axis_index(axis)], sems, axis, n)


def exchange_finish(src, copies, slots, axis, n):
    wait_recv(copies)
    slots[lax.axis_index(axis)] = src[...]
    total = slots[0]
    for k in range(1, n):
        total = total + slots[k]
    wait_send(copies)
    return total


def mix_kernel(subjects, nf, ns, ring, proj_ref, vg_ref, wg_ref, wts_ref, mix_ref, mask_ref,
               mix_out, hg_out, wts_out, wgl_out, basis_out, vg_out,
               part, mine, full, vslots, mslots, msend, spread, p_sem, g_sem, v_sem, m_sem):
    size = mix_ref.shape[0]
    greet((("feat", nf), ("subj", ns)))
    vcopies = exchange_start(vg_ref, vslots, v_sem, "feat", nf)
    if ring:
        copies = scatter_start(proj_ref, part, p_sem, "feat", nf)
    vgram = exchange_finish(vg_ref, vcopies, vslots, "feat", nf)
    vg_out[...] = vgram
    mix_inv = spd_inverse(vgram * wg_ref[...])
    if ring:
        scatter_finish(proj_ref, copies, part, mine, full, g_sem, "feat", nf)
        proj = full[...]
    else:
        proj = proj_ref[...]
    mask = mask_ref[...]
    wts = wts_ref[...]
    mixed = dot(mix_ref[...], proj * dot(wts, mask, TN))
    for s in range(subjects):
        spread[s * size : (s + 1) * size, :] = mixed * mask[s : s + 1, :]
    gram = dot(spread[...], mixed, NT)
    cross = dot(spread[...], proj, NT)
    eye = (lax.broadcasted_iota(jnp.int32, (size, size), 0)
           == lax.broadcasted_iota(jnp.int32, (size, size), 1)).astype(F32)
    uppers, lowers, scales = [], [], []
    for s in range(subjects):
        g = gram[s * size : (s + 1) * size, :]
        scale = jnp.sum(jnp.sum(g * eye, axis=1, keepdims=True), axis=0, keepdims=True) + 1e-06
        scales.append(scale)
        uppers.append(g / scale)
        lowers.append(eye)
    for step in range(NS_ITERS):
        for s in range(subjects):
            low_up = uppers[s] if step == 0 else dot(lowers[s], uppers[s])
            middle = 1.5 * eye - 0.5 * low_up
            lowers[s] = middle if step == 0 else dot(middle, lowers[s])
            if step < NS_ITERS - 1:
                uppers[s] = dot(uppers[s], middle)
    roots = [lowers[s] / jnp.sqrt(scales[s]) for s in range(subjects)]
    cores = [dot(roots[s], cross[s * size : (s + 1) * size, :]) for s in range(subjects)]
    msum = cores[0] * wts[0:1, :]
    for s in range(1, subjects):
        msum = msum + cores[s] * wts[s : s + 1, :]
    msend[...] = msum
    mcopies = exchange_start(msend, mslots, m_sem, "subj", ns)
    msum = exchange_finish(msend, mcopies, mslots, "subj", ns)
    mix_new = dot(msum, mix_inv)
    mix_out[...] = mix_new
    hgram = dot(mix_new, mix_new, TN)
    hg_out[...] = hgram
    turned = jnp.concatenate([dot(roots[s], mix_new) for s in range(subjects)], axis=0)
    ortho = dot(turned, spread[...], TN)
    target_row = lax.broadcasted_iota(jnp.int32, wts.shape, 0)
    target = jnp.zeros_like(wts)
    for s in range(subjects):
        target = jnp.where(target_row == s, jnp.sum(cores[s] * mix_new, axis=0, keepdims=True), target)
    wts_new = dot(target, spd_inverse(hgram * vgram))
    wts_out[...] = wts_new
    wgl_out[...] = dot(wts_new, wts_new, TN)
    basis_out[...] = ortho * dot(wts_new, mask, TN)


def factor_kernel(ns, ring, total_ref, wgl_ref, hg_ref, fac_out, wg_out, vgl_out,
                  part, mine, full, wslots, p_sem, g_sem, w_sem):
    greet((("subj", ns),))
    wcopies = exchange_start(wgl_ref, wslots, w_sem, "subj", ns)
    if ring:
        copies = scatter_start(total_ref, part, p_sem, "subj", ns)
    wgram = exchange_finish(wgl_ref, wcopies, wslots, "subj", ns)
    wg_out[...] = wgram
    inverse = spd_inverse(hg_ref[...] * wgram)
    if ring:
        scatter_finish(total_ref, copies, part, mine, full, g_sem, "subj", ns)
        total = full
    else:
        total = total_ref
    gram = jnp.zeros_like(wgram)
    width = total.shape[1]
    piece = min(width, 1024)
    for start in range(0, width, piece):
        value = dot(inverse, total[:, start : start + piece])
        fac_out[:, start : start + piece] = value
        gram = gram + dot(value, value, NT)
    vgl_out[...] = gram


def sems(n):
    return pltpu.SemaphoreType.DMA((2, max(n - 1, 1)))


def ring_scratch(shape, n, ring):
    rows = shape[0] // n if ring else SUBLANES
    cols = shape[1] if ring else 128
    return [
        pltpu.VMEM((max(n - 1, 1), rows, cols), F32),
        pltpu.VMEM((rows, cols), F32),
        pltpu.VMEM(shape if ring else (SUBLANES, 128), F32),
    ]


def mix_call(subjects, nf, ns, proj, vgl, wgram, wts, mix, mask):
    size = mix.shape[0]
    square = jax.ShapeDtypeStruct((size, size), F32)
    ring = nf > 1 and size % (SUBLANES * nf) == 0
    if not ring and nf > 1:
        proj = lax.psum(proj, "feat")
    vmem = pl.BlockSpec(memory_space=pltpu.VMEM)
    return pl.pallas_call(
        functools.partial(mix_kernel, subjects, nf, ns, ring),
        out_shape=(square, square, jax.ShapeDtypeStruct(wts.shape, F32), square,
                   jax.ShapeDtypeStruct(proj.shape, F32), square),
        in_specs=[vmem] * 6,
        out_specs=(vmem,) * 6,
        scratch_shapes=ring_scratch(proj.shape, nf, ring)
        + [
            pltpu.VMEM((nf, size, size), F32),
            pltpu.VMEM((ns, size, size), F32),
            pltpu.VMEM((size, size), F32),
            pltpu.VMEM((subjects * size, proj.shape[1]), F32),
            sems(nf), sems(nf), sems(nf), sems(ns),
        ],
        compiler_params=pltpu.CompilerParams(collective_id=0, has_side_effects=True),
        name="mix_step",
    )(proj, vgl, wgram, wts, mix, mask)


def factor_call(ns, total, wgl, hgram):
    size = total.shape[0]
    square = jax.ShapeDtypeStruct((size, size), F32)
    ring = ns > 1 and size % (SUBLANES * ns) == 0
    if not ring and ns > 1:
        total = lax.psum(total, "subj")
    vmem = pl.BlockSpec(memory_space=pltpu.VMEM)
    return pl.pallas_call(
        functools.partial(factor_kernel, ns, ring),
        out_shape=(jax.ShapeDtypeStruct(total.shape, F32), square, square),
        in_specs=[vmem] * 3,
        out_specs=(vmem,) * 3,
        scratch_shapes=ring_scratch(total.shape, ns, ring)
        + [pltpu.VMEM((ns, size, size), F32), sems(ns), sems(ns), sems(ns)],
        compiler_params=pltpu.CompilerParams(collective_id=1, has_side_effects=True),
        name="factor_step",
    )(total, wgl, hgram)


def solution(mesh):
    nf, ns = mesh.shape["feat"], mesh.shape["subj"]

    def per_device(records, feature_factor, mixing, weights, visits):
        subjects = weights.shape[0]
        padded = -(-subjects // SUBLANES) * SUBLANES
        mask = slot_rows(visits, records.shape[0], padded)
        wts = jnp.pad(weights, ((0, padded - subjects), (0, 0)))
        fac = feature_factor.T
        vgl = lax.dot_general(fac, fac, (NT, ((), ())), precision=HIGH, preferred_element_type=F32)
        wgram = lax.psum(
            jnp.dot(weights.T, weights, precision=HIGH, preferred_element_type=F32), "subj"
        )

        def step(_, state):
            fac, vgl, wgram, wts, mix = state
            proj = lax.dot_general(fac, records, (NT, ((), ())), precision=BIG, preferred_element_type=F32)
            mix, hgram, wts, wgl, basis, _ = mix_call(subjects, nf, ns, proj, vgl, wgram, wts, mix, mask)
            total = lax.dot_general(
                basis, records, (((1,), (0,)), ((), ())), precision=BIG, preferred_element_type=F32
            )
            fac, wgram, vgl = factor_call(ns, total, wgl, hgram)
            return fac, vgl, wgram, wts, mix

        fac, _, _, wts, mix = lax.fori_loop(0, ITERS, step, (fac, vgl, wgram, wts, mixing))
        return fac.T, mix, wts[:subjects]

    placed = (P("subj", "feat"), P("feat", None), P(), P("subj", None), P("subj"))
    return jax.shard_map(
        per_device,
        mesh=mesh,
        in_specs=placed,
        out_specs=(P("feat", None), P(), P("subj", None)),
        check_vma=False,
    )
```

time: 580 us -> 334 us (0.58)
  Pallas kernels: 0 us -> 222 us
  blocking collectives: 197 us -> 25.5 us
  other arithmetic: 109 us -> 1.57 us
  matrix products: 163 us -> 74.3 us
  waiting for transfers between devices: 86 us -> 0 us
  between operations: 15.9 us -> 0.66 us
    pallas_call x0 -> x6, Pallas kernels: none -> 222 us  [the longest x3 124 us: mix_call(): pl.pallas_call(functools.partial(mix_kernel, subjects, nf, ns, ring), out...]
    psum x9 -> x1, blocking collectives: 197 us -> 25.5 us  [per_device(): lax.psum(jnp.dot(weights.T, weights, precision=HIGH, preferred_element_ty...]
    another operation x47 -> x1, other arithmetic: 109 us -> 0.83 us  [the longest x28 58.7 us: solve_gram(): factor = jnp.linalg.cholesky(gram)]
    psum x6 -> x0, waiting for transfers between devices: 85.9 us -> none  [the longest x3 62.7 us: per_device(): total, wgram_new = lax.psum((local_total, local_wgram_new), 'subj')]
    dot_general x110 -> x8, matrix products: 149 us -> 74.3 us  [the longest x3 36.5 us: step(): lax.dot_general(basis, records, (((1,), (0,)), ((), ())), precision=BIG,...]
    another operation x18 -> x0, matrix products: 13.3 us -> none  [solve_gram(): return jax.scipy.linalg.cho_solve((factor, True), rhs.T).T]
  transfers between devices with their start and end apart: 6 -> 0, of which waited for: 6 -> 0; matrix products, arithmetic and copies ran while one was open for 11% -> 0% of each run, Pallas kernels for 0% -> 0%
where the time goes in v1:
time: 334 us; the launch traced here: 333 us
  Pallas kernels  222 us (66%)
  matrix products  74.3 us (22%)
  blocking collectives  25.5 us (8%)
  local copies, waits for them, and re-layouts  8.44 us (3%)
    pallas_call x3, Pallas kernels, mix_call(): pl.pallas_call(functools.partial(mix_kernel, subjects, nf, ns, ring), out...  124 us
    pallas_call x3, Pallas kernels, factor_call(): pl.pallas_call(functools.partial(factor_kernel, ns, ring), out_shape=(jax...  97.9 us
    dot_general x3, matrix products, step(): lax.dot_general(basis, records, (((1,), (0,)), ((), ())), precision=BIG,...  36.5 us
    dot_general x3, matrix products, step(): lax.dot_general(fac, records, (NT, ((), ())), precision=BIG, preferred_el...  35.8 us
    psum x1, blocking collectives, per_device(): lax.psum(jnp.dot(weights.T, weights, precision=HIGH, preferred_element_ty...  25.5 us

profile of v1, /device:TPU:0, one launch (start us, length us, event | category | flops | bytes accessed | tf_op | source)
XLA Modules:
  0.0 332.9 jit_solution(2893774757811744530)
XLA Ops:
  0.6 0.8 copy.34
  1.4 1.2 copy.33
  2.6 0.8 reduce-window.8
  3.4 0.7 bitcast_subtract_fusion
  4.1 0.1 fusion
  4.2 0.7 pad.11
  4.9 1.0 fusion.4
  5.9 25.5 %psum.7 = f32[64,64]{1,0:T(8,128)S(1)} all-reduce(f32[64,64]{1,0:T(8,128)S(1)} %fusion.4), channel_id=1, replica_groups=mesh['subj'=8,'feat'=4] {'subj'}, use_global_device_ids=true, to_apply=%region_0.0 | all-reduce | flops 4096 | bytes 32768 | tf_op jit(solution)/shard_map/psum | solution.py:284
  31.4 1.0 fusion.3
  32.4 298.4 %while.18 = (s32[]{:T(128)}, f32[64,4096]{1,0:T(8,128)S(1)}, f32[64,64]{1,0:T(8,128)S(1)}, f32[64,64]{1,0:T(8,128)S(1)}, f32[8,64]{1,0:T(8,128)S(1)}, /*index=5*...) while((s32[]{:T(128)}, f32[64,4096]{1,0:T(8,128)S(1)}, ...), condition=%wide.region_3.4_spmd, body=%wide.region_2.3_spmd.sunk | while | flops 3221225472 | bytes 36212828 | solution.py:298
  32.4 0.6 copy.36.wts_ref
  33.0 0.6 copy.37.mix_ref
  33.6 11.9 %fusion.23.proj_ref = f32[64,1024]{1,0:T(8,128)} fusion(f32[64,4096]{1,0:T(8,128)S(1)} %get-tuple-element.149, f32[1024,4096]{1,0:T(8,128)} %get-tuple-element.163), kind=kOutput, calls=%fused_computation.5.clone.1 | convolution fusion | flops 1610612736 | bytes 18087936 | tf_op jit(solution)/shard_map/while/body/eval_jaxpr/dot_general | solution.py:290
  45.6 41.0 %mix_step.1 = (f32[64,64]{1,0:T(8,128)S(1)}, f32[64,64]{1,0:T(8,128)}, f32[8,64]{1,0:T(8,128)S(1)}, f32[64,64]{1,0:T(8,128)}, f32[64,1024]{1,0:T(8,128)}, /*index=5*/f32[64,64]{1,0:T(8,128)}) custom-call(f32[64,1024]{1,0:T(8,128)} %fusion.23.proj_ref, f32[64,64]{1,0:T(8,128)S(1)} %get-tuple-element.150.vg_ref, f32[64,64]{1,0:T(8,128)S(1)} %get-tuple-element.151.wg_ref, ...), custom_call_target="tpu_custom_call" | custom-call | tf_op jit(solution)/shard_map/while/body/eval_jaxpr/mix_step/pallas_call | solution.py:236
  86.6 12.2 %fusion.24.total_ref = f32[64,4096]{1,0:T(8,128)} fusion(f32[64,1024]{1,0:T(8,128)} %get-tuple-element.131, f32[1024,4096]{1,0:T(8,128)} %get-tuple-element.163), kind=kOutput, calls=%fused_computation.6.clone.1 | convolution fusion | flops 1610612736 | bytes 18087936 | tf_op jit(solution)/shard_map/while/body/eval_jaxpr/dot_general | solution.py:292
  98.7 32.7 %factor_step.1 = (f32[64,4096]{1,0:T(8,128)S(1)}, f32[64,64]{1,0:T(8,128)S(1)}, f32[64,64]{1,0:T(8,128)S(1)}) custom-call(f32[64,4096]{1,0:T(8,128)} %fusion.24.total_ref, f32[64,64]{1,0:T(8,128)} %get-tuple-element.132.wgl_ref, f32[64,64]{1,0:T(8,128)} %get-tuple-element.133.hg_ref), custom_call_target="tpu_custom_call" | custom-call | tf_op jit(solution)/shard_map/while/body/eval_jaxpr/factor_step/pallas_call | solution.py:262
  131.5 0.6 copy.36.wts_ref
  132.1 0.6 copy.37.mix_ref
  132.7 11.9 %fusion.23.proj_ref = f32[64,1024]{1,0:T(8,128)} fusion(f32[64,4096]{1,0:T(8,128)S(1)} %get-tuple-element.149, f32[1024,4096]{1,0:T(8,128)} %get-tuple-element.163), kind=kOutput, calls=%fused_computation.5.clone.1 | convolution fusion | flops 1610612736 | bytes 18087936 | tf_op jit(solution)/shard_map/while/body/eval_jaxpr/dot_general | solution.py:290
  144.7 41.6 %mix_step.1 = (f32[64,64]{1,0:T(8,128)S(1)}, f32[64,64]{1,0:T(8,128)}, f32[8,64]{1,0:T(8,128)S(1)}, f32[64,64]{1,0:T(8,128)}, f32[64,1024]{1,0:T(8,128)}, /*index=5*/f32[64,64]{1,0:T(8,128)}) custom-call(f32[64,1024]{1,0:T(8,128)} %fusion.23.proj_ref, f32[64,64]{1,0:T(8,128)S(1)} %get-tuple-element.150.vg_ref, f32[64,64]{1,0:T(8,128)S(1)} %get-tuple-element.151.wg_ref, ...), custom_call_target="tpu_custom_call" | custom-call | tf_op jit(solution)/shard_map/while/body/eval_jaxpr/mix_step/pallas_call | solution.py:236
  186.3 12.2 %fusion.24.total_ref = f32[64,4096]{1,0:T(8,128)} fusion(f32[64,1024]{1,0:T(8,128)} %get-tuple-element.131, f32[1024,4096]{1,0:T(8,128)} %get-tuple-element.163), kind=kOutput, calls=%fused_computation.6.clone.1 | convolution fusion | flops 1610612736 | bytes 18087936 | tf_op jit(solution)/shard_map/while/body/eval_jaxpr/dot_general | solution.py:292
  198.5 32.6 %factor_step.1 = (f32[64,4096]{1,0:T(8,128)S(1)}, f32[64,64]{1,0:T(8,128)S(1)}, f32[64,64]{1,0:T(8,128)S(1)}) custom-call(f32[64,4096]{1,0:T(8,128)} %fusion.24.total_ref, f32[64,64]{1,0:T(8,128)} %get-tuple-element.132.wgl_ref, f32[64,64]{1,0:T(8,128)} %get-tuple-element.133.hg_ref), custom_call_target="tpu_custom_call" | custom-call | tf_op jit(solution)/shard_map/while/body/eval_jaxpr/factor_step/pallas_call | solution.py:262
  231.1 0.6 copy.36.wts_ref
  231.7 0.6 copy.37.mix_ref
  232.3 11.9 %fusion.23.proj_ref = f32[64,1024]{1,0:T(8,128)} fusion(f32[64,4096]{1,0:T(8,128)S(1)} %get-tuple-element.149, f32[1024,4096]{1,0:T(8,128)} %get-tuple-element.163), kind=kOutput, calls=%fused_computation.5.clone.1 | convolution fusion | flops 1610612736 | bytes 18087936 | tf_op jit(solution)/shard_map/while/body/eval_jaxpr/dot_general | solution.py:290
  244.3 41.8 %mix_step.1 = (f32[64,64]{1,0:T(8,128)S(1)}, f32[64,64]{1,0:T(8,128)}, f32[8,64]{1,0:T(8,128)S(1)}, f32[64,64]{1,0:T(8,128)}, f32[64,1024]{1,0:T(8,128)}, /*index=5*/f32[64,64]{1,0:T(8,128)}) custom-call(f32[64,1024]{1,0:T(8,128)} %fusion.23.proj_ref, f32[64,64]{1,0:T(8,128)S(1)} %get-tuple-element.150.vg_ref, f32[64,64]{1,0:T(8,128)S(1)} %get-tuple-element.151.wg_ref, ...), custom_call_target="tpu_custom_call" | custom-call | tf_op jit(solution)/shard_map/while/body/eval_jaxpr/mix_step/pallas_call | solution.py:236
  286.1 12.2 %fusion.24.total_ref = f32[64,4096]{1,0:T(8,128)} fusion(f32[64,1024]{1,0:T(8,128)} %get-tuple-element.131, f32[1024,4096]{1,0:T(8,128)} %get-tuple-element.163), kind=kOutput, calls=%fused_computation.6.clone.1 | convolution fusion | flops 1610612736 | bytes 18087936 | tf_op jit(solution)/shard_map/while/body/eval_jaxpr/dot_general | solution.py:292
  298.3 32.5 %factor_step.1 = (f32[64,4096]{1,0:T(8,128)S(1)}, f32[64,64]{1,0:T(8,128)S(1)}, f32[64,64]{1,0:T(8,128)S(1)}) custom-call(f32[64,4096]{1,0:T(8,128)} %fusion.24.total_ref, f32[64,64]{1,0:T(8,128)} %get-tuple-element.132.wgl_ref, f32[64,64]{1,0:T(8,128)} %get-tuple-element.133.hg_ref), custom_call_target="tpu_custom_call" | custom-call | tf_op jit(solution)/shard_map/while/body/eval_jaxpr/factor_step/pallas_call | solution.py:262
  330.8 0.6 slice.3
  331.4 1.0 copy.38
  332.3 0.6 copy.39
  (1 shorter events, 0.0 us)
